TPU v7x, 256 devices: a whole 4x4x8 slice. The times are simulated.
256 devices in a mesh: harm: 64 (over y, z, core), node: 4 (over x).
Axes of the slice: x: 4, y: 4, z: 8, core: 2. Of those that a mesh axis runs over, the one named last changes fastest.
Arguments:
- state: float32 [2, 128, 512, 128], P(None, 'harm', 'node'), may hold values from -0.6 to 0.6
- source: float32 [2, 128, 512, 128], P(None, 'harm', 'node'), may hold values from -6 to 6
- capacity: float32 [512, 128], P('node'), may hold values from 0.05 to 0.5
- row_shift: int32 [512], P('node'), may hold values from 0 to 3
- device_type: int32 [512, 128], P('node'), may hold values from 0 to 3
- device_table: float32 [3, 4], replicated, may hold values from 0.5 to 2
- precond: float32 [2, 128, 128, 128], P(None, 'harm'), may hold values from -1 to 1, as said below
Outputs:
- update: float32 [2, 128, 512, 128], P(None, 'harm', 'node')
- resid: float32 [2, 128, 512, 128], P(None, 'harm', 'node')
Inputs may be any that keep to these rules, and one draw needn't show every extreme that they name: precond[0, k] is 1/6 on the diagonal plus a full-rank fluctuation; precond[1, k] is a full-rank fluctuation.
All inputs are finite; a program needn't handle non-finite values.
Results may differ from a plain program's by a relative error of at most 0.00011.
Values sent between devices are 32-bit elements; how exact they have to be, the bound alone decides.
A program may use at most 64 MiB of HBM per device.

v0:
```python
import functools
import jax
import jax.numpy as jnp
from jax import lax
from jax.sharding import Mesh
from jax.sharding import PartitionSpec as P

ITERS = 3
TYPES = 4
SHIFTS = 4
HARM = ("harm_0", "harm_1", "harm_2")
HARM_NODE = ("harm_0", "harm_1", "harm_2", "node")
omega_step = 0.05
top = lax.Precision.HIGHEST


def extended(cells, sides, width):
    for axis, dim in sides:
        count = lax.axis_size(axis)
        ends = count - 1
        head = lax.slice_in_dim(cells, 0, width, axis=dim)
        tail = lax.slice_in_dim(cells, cells.shape[dim] - width, cells.shape[dim], axis=dim)
        cells = jnp.concatenate(
            [
                lax.ppermute(tail, axis, [(i, (i + 1) % count) for i in range(ends)]),
                cells,
                lax.ppermute(head, axis, [((i + 1) % count, i) for i in range(ends)]),
            ],
            axis=dim,
        )
    return cells


def by_axis(shard, axes):
    return functools.reduce(lax.psum, axes, shard)


def small_solve(gram, right):
    lower = jnp.linalg.cholesky(gram)
    order = gram.shape[0]
    forward = []
    for column in range(order):
        value = right[column]
        for member in range(column):
            value = value - lower[column, member] * forward[member]
        forward.append(value / lower[column, column])
    result = [None] * order
    for column in reversed(range(order)):
        value = forward[column]
        for member in range(column + 1, order):
            value = value - lower[member, column] * result[member]
        result[column] = value / lower[column, column]
    return result


def tables(harmonics, samples):
    waves = jnp.arange(harmonics, dtype=jnp.int32)
    moments = jnp.arange(samples, dtype=jnp.int32)
    phase = (moments[:, None] * waves[None, :] % samples).astype(jnp.float32) * (
        2.0 * jnp.pi / samples
    )
    cosine = jnp.cos(phase)
    sine = jnp.sin(phase)
    inverse = jnp.concatenate([cosine, -sine], axis=1)
    weights = jnp.where(waves == 0, 1.0, 2.0).astype(jnp.float32) / samples
    forward = jnp.concatenate([cosine.T * weights[:, None], -sine.T * weights[:, None]], axis=0)
    return (inverse, forward)


def stencil(field, above, below, capacity, shifts, waves):
    left_side = jnp.roll(field, 1, axis=3)
    right_side = jnp.roll(field, -1, axis=3)
    skewed = jnp.zeros_like(field)
    for amount in range(SHIFTS):
        picked = (shifts == amount).astype(jnp.float32)[None, None, :, None]
        skewed = skewed + picked * jnp.roll(above, -amount, axis=3)
    result = 4.0 * field - left_side - right_side - skewed - below
    reactive = omega_step * waves.astype(jnp.float32)[:, None, None] * capacity[None]
    return result + jnp.stack([-reactive * field[1], reactive * field[0]])


def precondition(field, blocks):
    real_part = jnp.einsum("krd,kcd->krc", field[0], blocks[0], precision=top) - jnp.einsum(
        "krd,kcd->krc", field[1], blocks[1], precision=top
    )
    imag_part = jnp.einsum("krd,kcd->krc", field[0], blocks[1], precision=top) + jnp.einsum(
        "krd,kcd->krc", field[1], blocks[0], precision=top
    )
    return jnp.stack([real_part, imag_part])


def body(state, source, capacity, row_shift, device_type, device_table, precond):
    groups = lax.axis_size(HARM)
    place = lax.axis_index(HARM)
    local_harm = state.shape[1]
    block_rows = state.shape[2]
    columns = state.shape[3]
    harmonics = local_harm * groups
    samples = 2 * harmonics
    own_rows = block_rows // groups
    inverse, forward = tables(harmonics, samples)
    kinds = lax.dynamic_slice_in_dim(device_type, place * own_rows, own_rows, 0).reshape(-1)
    params = jnp.zeros((3, kinds.shape[0]), jnp.float32)
    for member in range(TYPES):
        params = (
            params
            + (kinds == member).astype(jnp.float32)[None, :] * device_table[:, member][:, None]
        )
    linear, amplitude, slope = (params[0], params[1], params[2])

    def time_of(spectrum):
        return jnp.dot(
            inverse,
            spectrum.reshape(2 * harmonics, -1),
            precision=top,
            preferred_element_type=jnp.float32,
        )

    def spectrum_of(signal):
        return jnp.dot(forward, signal, precision=top, preferred_element_type=jnp.float32).reshape(
            2, harmonics, own_rows, columns
        )

    def currents(spectrum):
        voltage = time_of(spectrum)
        bent = jnp.tanh(slope * voltage)
        flow = linear * voltage + amplitude * bent
        slopes_now = linear + amplitude * slope * (1.0 - bent * bent)
        return (spectrum_of(flow), slopes_now)

    field_state, field_source = (state, source)
    waves = place * local_harm + jnp.arange(local_harm, dtype=jnp.int32)

    def sides(field):
        padded = extended(field, (("node", 2),), 1)
        return (padded[:, :, :-2], padded[:, :, 2:])

    def across(field, local):
        moved = lax.all_to_all(field, HARM, split_axis=2, concat_axis=1, tiled=True)
        result, extra = local(moved)
        return (lax.all_to_all(result, HARM, split_axis=1, concat_axis=2, tiled=True), extra)

    def operator(field):
        above, below = sides(field)
        return stencil(field, above, below, capacity, row_shift, waves)

    spec_flow, slopes = across(field_state, currents)
    resid = operator(field_state) + spec_flow - field_source

    def linear_part(spectrum):
        return (spectrum_of(slopes * time_of(spectrum)), slopes)

    start = -resid
    beta = jnp.sqrt(by_axis(jnp.sum(start * start), HARM_NODE))
    basis = [start / beta]
    directions = []
    columns_h = []
    for iteration in range(ITERS):
        direction = precondition(basis[iteration], precond)
        directions.append(direction)
        coupled, unused = across(direction, linear_part)
        image = operator(direction) + coupled
        locals_dot = jnp.stack([jnp.sum(basis[member] * image) for member in range(iteration + 1)])
        totals, square = (
            by_axis(locals_dot, HARM_NODE),
            by_axis(jnp.sum(image * image), HARM_NODE),
        )
        heights = [totals[member] for member in range(iteration + 1)]
        for earlier in range(iteration + 1):
            image = image - heights[earlier] * basis[earlier]
        length = jnp.sqrt(square - jnp.sum(totals * totals))
        columns_h.append(
            jnp.stack(heights + [length] + [jnp.zeros((), jnp.float32)] * (ITERS - 1 - iteration))
        )
        if iteration + 1 < ITERS:
            basis.append(image / length)
    hess = jnp.stack(columns_h, axis=1)
    gram = jnp.dot(hess.T, hess, precision=top)
    coeffs = small_solve(gram, beta * hess[0])
    update = jnp.zeros_like(field_state)
    for iteration in range(ITERS):
        update = update + coeffs[iteration] * directions[iteration]
    return (update, resid)


def solution(mesh):
    finer = Mesh(
        mesh.devices.reshape(4, 8, 2, mesh.shape["node"]), ("harm_0", "harm_1", "harm_2", "node")
    )
    return jax.shard_map(
        body,
        mesh=finer,
        in_specs=(
            P(None, HARM, "node", None),
            P(None, HARM, "node", None),
            P("node", None),
            P("node"),
            P("node", None),
            P(),
            P(None, HARM, None, None),
        ),
        out_specs=(P(None, HARM, "node", None), P(None, HARM, "node", None)),
        check_vma=False,
    )
```

profile of v0, /device:TPU:2, one launch (start us, length us, event | category | flops | bytes accessed | tf_op | source)
XLA Modules:
  0.0 376.9 jit_solution(4590156179275727498)
XLA Ops:
  9.1 12.2 %all-to-all-start = ((f32[2,2,128,128]{3,1,0,2:T(2,128)}), f32[2,2,128,128]{3,1,0,2:T(2,128)S(1)}, u32[]{:S(2)}, u32[]{:S(2)}) async-start(f32[2,2,128,128]{3,1,0,2:T(2,128)} %copy.23), calls=%async_computation | async-start | bytes 524288 | tf_op jit(solution)/shard_map/all_to_all | solution.py:139
  24.8 8.5 %all-to-all-done = f32[2,2,128,128]{3,1,0,2:T(2,128)S(1)} async-done(((f32[2,2,128,128]{3,1,0,2:T(2,128)}), f32[2,2,128,128]{3,1,0,2:T(2,128)S(1)}, u32[]{:S(2)}, u32[]{:S(2)}) %all-to-all-start) | async-done | bytes 262176 | tf_op jit(solution)/shard_map/all_to_all | solution.py:139
  35.2 6.0 %all-to-all-start.1 = ((f32[2,128,2,128]{3,2,0,1:T(2,128)}), f32[2,128,2,128]{3,2,0,1:T(2,128)S(1)}, u32[]{:S(2)}, u32[]{:S(2)}) async-start(f32[2,128,2,128]{3,2,0,1:T(2,128)} %copy.25), calls=%async_computation.1 | async-start | bytes 524288 | tf_op jit(solution)/shard_map/all_to_all | solution.py:141
  42.3 10.9 %all-to-all-done.1 = f32[2,128,2,128]{3,2,0,1:T(2,128)S(1)} async-done(((f32[2,128,2,128]{3,2,0,1:T(2,128)}), f32[2,128,2,128]{3,2,0,1:T(2,128)S(1)}, u32[]{:S(2)}, u32[]{:S(2)}) %all-to-all-start.1) | async-done | bytes 262176 | tf_op jit(solution)/shard_map/all_to_all | solution.py:141
  56.3 10.9 %psum.196 = f32[]{:T(128)} all-reduce(f32[]{:T(128)} %get-tuple-element.41), channel_id=1, replica_groups=mesh['harm_0'=4,'harm_1'=8,'harm_2'=2,'node'=4] {'harm_0'}, use_global_device_ids=true, to_apply=%region_1.2 | all-reduce | flops 1 | bytes 8 | tf_op jit(solution)/shard_map/psum | solution.py:35
  67.2 15.5 %psum.197 = f32[]{:T(128)} all-reduce(f32[]{:T(128)} %psum.196), channel_id=1, replica_groups=mesh['harm_0'=4,'harm_1'=8,'harm_2'=2,'node'=4] {'harm_1'}, use_global_device_ids=true, to_apply=%region_2.3 | all-reduce | flops 1 | bytes 8 | tf_op jit(solution)/shard_map/psum | solution.py:35
  85.8 9.2 %psum.199 = f32[]{:T(128)} all-reduce(f32[]{:T(128)} %psum.198), channel_id=1, replica_groups=mesh['harm_0'=4,'harm_1'=8,'harm_2'=2,'node'=4] {'node'}, use_global_device_ids=true, to_apply=%region_4.5 | all-reduce | flops 1 | bytes 8 | tf_op jit(solution)/shard_map/psum | solution.py:35
  99.2 5.6 %all-to-all-start.2 = ((f32[2,2,128,128]{3,1,0,2:T(2,128)}), f32[2,2,128,128]{3,1,0,2:T(2,128)S(1)}, u32[]{:S(2)}, u32[]{:S(2)}) async-start(f32[2,2,128,128]{3,1,0,2:T(2,128)} %copy.27), calls=%async_computation.2 | async-start | bytes 524288 | tf_op jit(solution)/shard_map/all_to_all | solution.py:139
  105.0 11.8 %all-to-all-done.2 = f32[2,2,128,128]{3,1,0,2:T(2,128)S(1)} async-done(((f32[2,2,128,128]{3,1,0,2:T(2,128)}), f32[2,2,128,128]{3,1,0,2:T(2,128)S(1)}, u32[]{:S(2)}, u32[]{:S(2)}) %all-to-all-start.2) | async-done | bytes 262176 | tf_op jit(solution)/shard_map/all_to_all | solution.py:139
  118.7 6.0 %all-to-all-start.3 = ((f32[2,128,2,128]{3,2,0,1:T(2,128)}), f32[2,128,2,128]{3,2,0,1:T(2,128)S(1)}, u32[]{:S(2)}, u32[]{:S(2)}) async-start(f32[2,128,2,128]{3,2,0,1:T(2,128)} %copy.29), calls=%async_computation.3 | async-start | bytes 524288 | tf_op jit(solution)/shard_map/all_to_all | solution.py:141
  140.1 11.0 %all-reduce.8 = (f32[]{:T(128)}, f32[1]{0:T(128)}) all-reduce(f32[]{:T(128)} %get-tuple-element.10, f32[1]{0:T(128)} %bitcast.26), channel_id=1, replica_groups=mesh['harm_0'=4,'harm_1'=8,'harm_2'=2,'node'=4] {'harm_0'}, use_global_device_ids=true, to_apply=%region_11.12 | all-reduce | flops 2 | bytes 16 | tf_op jit(solution)/shard_map/psum | solution.py:35
  151.1 17.0 %all-reduce.2 = (f32[]{:T(128)}, f32[1]{0:T(128)}) all-reduce(f32[]{:T(128)} %get-tuple-element.31, f32[1]{0:T(128)} %get-tuple-element.32), channel_id=1, replica_groups=mesh['harm_0'=4,'harm_1'=8,'harm_2'=2,'node'=4] {'harm_1'}, use_global_device_ids=true, to_apply=%region_12.13 | all-reduce | flops 2 | bytes 16 | tf_op jit(solution)/shard_map/psum | solution.py:35
  171.3 9.3 %all-reduce.5 = (f32[]{:T(128)}, f32[1]{0:T(128)}) all-reduce(f32[]{:T(128)} %get-tuple-element.37, f32[1]{0:T(128)} %get-tuple-element.38), channel_id=1, replica_groups=mesh['harm_0'=4,'harm_1'=8,'harm_2'=2,'node'=4] {'node'}, use_global_device_ids=true, to_apply=%region_14.15 | all-reduce | flops 2 | bytes 16 | tf_op jit(solution)/shard_map/psum | solution.py:35
  191.3 11.8 %all-to-all-done.4 = f32[2,2,128,128]{3,1,0,2:T(2,128)S(1)} async-done(((f32[2,2,128,128]{3,1,0,2:T(2,128)}), f32[2,2,128,128]{3,1,0,2:T(2,128)S(1)}, u32[]{:S(2)}, u32[]{:S(2)}) %all-to-all-start.4) | async-done | bytes 262176 | tf_op jit(solution)/shard_map/all_to_all | solution.py:139
  205.0 6.3 %all-to-all-start.5 = ((f32[2,128,2,128]{3,2,0,1:T(2,128)}), f32[2,128,2,128]{3,2,0,1:T(2,128)}, u32[]{:S(2)}, u32[]{:S(2)}) async-start(f32[2,128,2,128]{3,2,0,1:T(2,128)} %copy.34), calls=%async_computation.5 | async-start | bytes 524288 | tf_op jit(solution)/shard_map/all_to_all | solution.py:141
  229.5 11.1 %all-reduce.7 = (f32[]{:T(128)}, f32[2]{0:T(128)S(1)}) all-reduce(f32[]{:T(128)} %get-tuple-element.7, f32[2]{0:T(128)S(1)} %pad_maximum_fusion.22), channel_id=1, replica_groups=mesh['harm_0'=4,'harm_1'=8,'harm_2'=2,'node'=4] {'harm_0'}, use_global_device_ids=true, to_apply=%region_22.23 | all-reduce | flops 3 | bytes 24 | tf_op jit(solution)/shard_map/psum | solution.py:35
  240.6 17.5 %all-reduce.1 = (f32[]{:T(128)}, f32[2]{0:T(128)S(1)}) all-reduce(f32[]{:T(128)} %get-tuple-element.29, f32[2]{0:T(128)S(1)} %get-tuple-element.30), channel_id=1, replica_groups=mesh['harm_0'=4,'harm_1'=8,'harm_2'=2,'node'=4] {'harm_1'}, use_global_device_ids=true, to_apply=%region_23.24 | all-reduce | flops 3 | bytes 24 | tf_op jit(solution)/shard_map/psum | solution.py:35
  261.2 8.0 %all-reduce.4 = (f32[]{:T(128)}, f32[2]{0:T(128)S(1)}) all-reduce(f32[]{:T(128)} %get-tuple-element.35, f32[2]{0:T(128)S(1)} %get-tuple-element.36), channel_id=1, replica_groups=mesh['harm_0'=4,'harm_1'=8,'harm_2'=2,'node'=4] {'node'}, use_global_device_ids=true, to_apply=%region_25.26 | all-reduce | flops 3 | bytes 24 | tf_op jit(solution)/shard_map/psum | solution.py:35
  276.6 5.8 %all-to-all-start.6 = ((f32[2,2,128,128]{3,1,0,2:T(2,128)}), f32[2,2,128,128]{3,1,0,2:T(2,128)S(1)}, u32[]{:S(2)}, u32[]{:S(2)}) async-start(f32[2,2,128,128]{3,1,0,2:T(2,128)} %copy.37), calls=%async_computation.6 | async-start | bytes 524288 | tf_op jit(solution)/shard_map/all_to_all | solution.py:139
  284.6 9.8 %all-to-all-done.6 = f32[2,2,128,128]{3,1,0,2:T(2,128)S(1)} async-done(((f32[2,2,128,128]{3,1,0,2:T(2,128)}), f32[2,2,128,128]{3,1,0,2:T(2,128)S(1)}, u32[]{:S(2)}, u32[]{:S(2)}) %all-to-all-start.6) | async-done | bytes 262176 | tf_op jit(solution)/shard_map/all_to_all | solution.py:139
  296.2 6.3 %all-to-all-start.7 = ((f32[2,128,2,128]{3,2,0,1:T(2,128)}), f32[2,128,2,128]{3,2,0,1:T(2,128)}, u32[]{:S(2)}, u32[]{:S(2)}) async-start(f32[2,128,2,128]{3,2,0,1:T(2,128)} %copy.39), calls=%async_computation.7 | async-start | bytes 524288 | tf_op jit(solution)/shard_map/all_to_all | solution.py:141
  320.5 10.9 %all-reduce.6 = (f32[]{:T(128)}, f32[3]{0:T(128)S(1)}) all-reduce(f32[]{:T(128)} %get-tuple-element.3, f32[3]{0:T(128)S(1)} %pad_maximum_fusion.23), channel_id=1, replica_groups=mesh['harm_0'=4,'harm_1'=8,'harm_2'=2,'node'=4] {'harm_0'}, use_global_device_ids=true, to_apply=%region_35.36 | all-reduce | flops 4 | bytes 32 | tf_op jit(solution)/shard_map/psum | solution.py:35
  331.4 16.1 %all-reduce = (f32[]{:T(128)}, f32[3]{0:T(128)S(1)}) all-reduce(f32[]{:T(128)} %get-tuple-element.27, f32[3]{0:T(128)S(1)} %get-tuple-element.28), channel_id=1, replica_groups=mesh['harm_0'=4,'harm_1'=8,'harm_2'=2,'node'=4] {'harm_1'}, use_global_device_ids=true, to_apply=%region_36.37 | all-reduce | flops 4 | bytes 32 | tf_op jit(solution)/shard_map/psum | solution.py:35
  350.6 10.2 %all-reduce.3 = (f32[]{:T(128)}, f32[3]{0:T(128)S(1)}) all-reduce(f32[]{:T(128)} %get-tuple-element.33, f32[3]{0:T(128)S(1)} %get-tuple-element.34), channel_id=1, replica_groups=mesh['harm_0'=4,'harm_1'=8,'harm_2'=2,'node'=4] {'node'}, use_global_device_ids=true, to_apply=%region_38.39 | all-reduce | flops 4 | bytes 32 | tf_op jit(solution)/shard_map/psum | solution.py:35
  (193 shorter events, 112.7 us)
Async XLA Ops:
  1.4 23.2 %collective-permute-start = (f32[2,2,1,128]{3,2,1,0:T(1,128)S(1)}, f32[2,2,1,128]{3,2,1,0:T(1,128)S(1)}, u32[]{:S(2)}, u32[]{:S(2)}) collective-permute-start(f32[2,2,1,128]{3,2,1,0:T(1,128)S(1)} %get-tuple-element.69), channel_id=1, source_target_pairs={{0,1},{1,2},{2,3},{4,5},{5,6},{6,7},{8,9},{9,10},{10,11},{12,13},{... | collective-permute-start | bytes 6152 | tf_op jit(solution)/shard_map/ppermute | solution.py:25
  4.8 48.5 %collective-permute-start.1 = (f32[2,2,1,128]{3,2,1,0:T(1,128)S(1)}, f32[2,2,1,128]{3,2,1,0:T(1,128)S(1)}, u32[]{:S(2)}, u32[]{:S(2)}) collective-permute-start(f32[2,2,1,128]{3,2,1,0:T(1,128)S(1)} %get-tuple-element.70), channel_id=1, source_target_pairs={{1,0},{2,1},{3,2},{5,4},{6,5},{7,6},{9,8},{10,9},{11,10},{13,12},{... | collective-permute-start | bytes 6152 | tf_op jit(solution)/shard_map/ppermute | solution.py:27
  9.1 12.3 %copy-start.20 = (f32[3,4]{1,0:T(4,128)S(1)}, f32[3,4]{1,0:T(4,128)}, u32[]{:S(2)}) copy-start(f32[3,4]{1,0:T(4,128)} %param.12) | copy-start | bytes 148
  9.1 24.2 %all-to-all-start = ((f32[2,2,128,128]{3,1,0,2:T(2,128)}), f32[2,2,128,128]{3,1,0,2:T(2,128)S(1)}, u32[]{:S(2)}, u32[]{:S(2)}) async-start(f32[2,2,128,128]{3,1,0,2:T(2,128)} %copy.23), calls=%async_computation | async-start | bytes 524288 | tf_op jit(solution)/shard_map/all_to_all | solution.py:139
  21.3 1.6 copy-start
  35.2 18.0 %all-to-all-start.1 = ((f32[2,128,2,128]{3,2,0,1:T(2,128)}), f32[2,128,2,128]{3,2,0,1:T(2,128)S(1)}, u32[]{:S(2)}, u32[]{:S(2)}) async-start(f32[2,128,2,128]{3,2,0,1:T(2,128)} %copy.25), calls=%async_computation.1 | async-start | bytes 524288 | tf_op jit(solution)/shard_map/all_to_all | solution.py:141
  56.3 259.3 %copy-start.1 = (f32[2,2,128,128]{3,2,1,0:T(8,128)}, f32[2,2,128,128]{3,2,1,0:T(8,128)S(1)}, u32[]{:S(2)}) copy-start(f32[2,2,128,128]{3,2,1,0:T(8,128)S(1)} %get-tuple-element.42) | copy-start | bytes 786436
  99.2 17.6 %all-to-all-start.2 = ((f32[2,2,128,128]{3,1,0,2:T(2,128)}), f32[2,2,128,128]{3,1,0,2:T(2,128)S(1)}, u32[]{:S(2)}, u32[]{:S(2)}) async-start(f32[2,2,128,128]{3,1,0,2:T(2,128)} %copy.27), calls=%async_computation.2 | async-start | bytes 524288 | tf_op jit(solution)/shard_map/all_to_all | solution.py:139
  118.7 18.0 %all-to-all-start.3 = ((f32[2,128,2,128]{3,2,0,1:T(2,128)}), f32[2,128,2,128]{3,2,0,1:T(2,128)S(1)}, u32[]{:S(2)}, u32[]{:S(2)}) async-start(f32[2,128,2,128]{3,2,0,1:T(2,128)} %copy.29), calls=%async_computation.3 | async-start | bytes 524288 | tf_op jit(solution)/shard_map/all_to_all | solution.py:141
  124.7 7.0 %collective-permute-start.2 = (f32[2,2,1,128]{3,2,1,0:T(1,128)S(1)}, f32[2,2,1,128]{3,2,1,0:T(1,128)S(1)}, u32[]{:S(2)}, u32[]{:S(2)}) collective-permute-start(f32[2,2,1,128]{3,2,1,0:T(1,128)S(1)} %get-tuple-element.61), channel_id=1, source_target_pairs={{0,1},{1,2},{2,3},{4,5},{5,6},{6,7},{8,9},{9,10},{10,11},{12,13},{... | collective-permute-start | bytes 6152 | tf_op jit(solution)/shard_map/ppermute | solution.py:25
  128.7 8.2 %collective-permute-start.3 = (f32[2,2,1,128]{3,2,1,0:T(1,128)S(1)}, f32[2,2,1,128]{3,2,1,0:T(1,128)S(1)}, u32[]{:S(2)}, u32[]{:S(2)}) collective-permute-start(f32[2,2,1,128]{3,2,1,0:T(1,128)S(1)} %get-tuple-element.62), channel_id=1, source_target_pairs={{1,0},{2,1},{3,2},{5,4},{6,5},{7,6},{9,8},{10,9},{11,10},{13,12},{... | collective-permute-start | bytes 6152 | tf_op jit(solution)/shard_map/ppermute | solution.py:27
  185.6 17.6 %all-to-all-start.4 = ((f32[2,2,128,128]{3,1,0,2:T(2,128)}), f32[2,2,128,128]{3,1,0,2:T(2,128)S(1)}, u32[]{:S(2)}, u32[]{:S(2)}) async-start(f32[2,2,128,128]{3,1,0,2:T(2,128)} %copy.32), calls=%async_computation.4 | async-start | bytes 524288 | tf_op jit(solution)/shard_map/all_to_all | solution.py:139
  205.0 18.1 %all-to-all-start.5 = ((f32[2,128,2,128]{3,2,0,1:T(2,128)}), f32[2,128,2,128]{3,2,0,1:T(2,128)}, u32[]{:S(2)}, u32[]{:S(2)}) async-start(f32[2,128,2,128]{3,2,0,1:T(2,128)} %copy.34), calls=%async_computation.5 | async-start | bytes 524288 | tf_op jit(solution)/shard_map/all_to_all | solution.py:141
  211.3 6.8 %collective-permute-start.4 = (f32[2,2,1,128]{3,2,1,0:T(1,128)S(1)}, f32[2,2,1,128]{3,2,1,0:T(1,128)S(1)}, u32[]{:S(2)}, u32[]{:S(2)}) collective-permute-start(f32[2,2,1,128]{3,2,1,0:T(1,128)S(1)} %get-tuple-element.55), channel_id=1, source_target_pairs={{0,1},{1,2},{2,3},{4,5},{5,6},{6,7},{8,9},{9,10},{10,11},{12,13},{... | collective-permute-start | bytes 6152 | tf_op jit(solution)/shard_map/ppermute | solution.py:25
  214.4 10.0 %collective-permute-start.5 = (f32[2,2,1,128]{3,2,1,0:T(1,128)S(1)}, f32[2,2,1,128]{3,2,1,0:T(1,128)S(1)}, u32[]{:S(2)}, u32[]{:S(2)}) collective-permute-start(f32[2,2,1,128]{3,2,1,0:T(1,128)S(1)} %get-tuple-element.56), channel_id=1, source_target_pairs={{1,0},{2,1},{3,2},{5,4},{6,5},{7,6},{9,8},{10,9},{11,10},{13,12},{... | collective-permute-start | bytes 6152 | tf_op jit(solution)/shard_map/ppermute | solution.py:27
  223.1 1.3 copy-start.9
  223.1 1.3 copy-start.10
  276.6 17.8 %all-to-all-start.6 = ((f32[2,2,128,128]{3,1,0,2:T(2,128)}), f32[2,2,128,128]{3,1,0,2:T(2,128)S(1)}, u32[]{:S(2)}, u32[]{:S(2)}) async-start(f32[2,2,128,128]{3,1,0,2:T(2,128)} %copy.37), calls=%async_computation.6 | async-start | bytes 524288 | tf_op jit(solution)/shard_map/all_to_all | solution.py:139
  296.2 18.1 %all-to-all-start.7 = ((f32[2,128,2,128]{3,2,0,1:T(2,128)}), f32[2,128,2,128]{3,2,0,1:T(2,128)}, u32[]{:S(2)}, u32[]{:S(2)}) async-start(f32[2,128,2,128]{3,2,0,1:T(2,128)} %copy.39), calls=%async_computation.7 | async-start | bytes 524288 | tf_op jit(solution)/shard_map/all_to_all | solution.py:141
  302.6 6.7 %collective-permute-start.6 = (f32[2,2,1,128]{3,2,1,0:T(1,128)S(1)}, f32[2,2,1,128]{3,2,1,0:T(1,128)S(1)}, u32[]{:S(2)}, u32[]{:S(2)}) collective-permute-start(f32[2,2,1,128]{3,2,1,0:T(1,128)S(1)} %get-tuple-element.49), channel_id=1, source_target_pairs={{0,1},{1,2},{2,3},{4,5},{5,6},{6,7},{8,9},{9,10},{10,11},{12,13},{... | collective-permute-start | bytes 6152 | tf_op jit(solution)/shard_map/ppermute | solution.py:25
  305.7 10.0 %collective-permute-start.7 = (f32[2,2,1,128]{3,2,1,0:T(1,128)S(1)}, f32[2,2,1,128]{3,2,1,0:T(1,128)S(1)}, u32[]{:S(2)}, u32[]{:S(2)}) collective-permute-start(f32[2,2,1,128]{3,2,1,0:T(1,128)S(1)} %get-tuple-element.50), channel_id=1, source_target_pairs={{1,0},{2,1},{3,2},{5,4},{6,5},{7,6},{9,8},{10,9},{11,10},{13,12},{... | collective-permute-start | bytes 6152 | tf_op jit(solution)/shard_map/ppermute | solution.py:27
  311.7 3.9 %copy-start.19 = (f32[1,2,128,128]{3,2,1,0:T(8,128)S(1)}, f32[1,2,128,128]{3,2,1,0:T(8,128)}, u32[]{:S(2)}) copy-start(f32[1,2,128,128]{3,2,1,0:T(8,128)} %get-tuple-element.72) | copy-start | bytes 393220
  314.4 1.3 copy-start.5
  314.4 1.3 copy-start.6
  (15 other events, 14.4 us)
where the time goes:
time: 379 us; the launch traced here: 377 us
  blocking collectives  159 us (42%)
  starting transfers between devices  77.5 us (20%)
  waiting for transfers between devices  55.9 us (15%)
  local copies, waits for them, and re-layouts  31.7 us (8%)
  other arithmetic  28.6 us (8%)
  between operations  16.3 us (4%)
  matrix products  7.83 us (2%)
    psum x16, blocking collectives, by_axis(): return functools.reduce(lax.psum, axes, shard)  159 us
    all_to_all x4, waiting for transfers between devices, across(): moved = lax.all_to_all(field, HARM, split_axis=2, concat_axis=1, tiled=True)  42 us
    all_to_all x4, starting transfers between devices, across(): moved = lax.all_to_all(field, HARM, split_axis=2, concat_axis=1, tiled=True)  29.3 us
    all_to_all x4, starting transfers between devices, across(): lax.all_to_all(result, HARM, split_axis=1, concat_axis=2, tiled=True)  24.6 us
    all_to_all x4, waiting for transfers between devices, across(): lax.all_to_all(result, HARM, split_axis=1, concat_axis=2, tiled=True)  13.9 us
    slice x18, local copies, waits for them, and re-layouts, stencil(): skewed = skewed + picked * jnp.roll(above, -amount, axis=3)  12 us
    ppermute x4, starting transfers between devices, extended(): lax.ppermute(head, axis, [((i + 1) % count, i) for i in range(ends)])  11.8 us
    ppermute x4, starting transfers between devices, extended(): lax.ppermute(tail, axis, [(i, (i + 1) % count) for i in range(ends)])  11.7 us
  transfers between devices with their start and end apart: 16, of which 8 were waited for; matrix products, arithmetic and copies ran while one was open for 7% of the time, Pallas kernels for 0%

commit v1 on v0

--- a/solution.py
+++ b/solution.py
@@ -12,6 +12,15 @@
 HARM_NODE = ("harm_0", "harm_1", "harm_2", "node")
 omega_step = 0.05
 top = lax.Precision.HIGHEST
+
+
+def register_the_panel(sheet, net_axis):
+    return jnp.concatenate(
+        lax.all_to_all(
+            jnp.stack(jnp.split(sheet, lax.axis_size(net_axis), axis=1), axis=0), net_axis, 0, 0
+        ),
+        axis=2,
+    )
 
 
 def extended(cells, sides, width):
@@ -138,7 +147,7 @@
     def across(field, local):
         moved = lax.all_to_all(field, HARM, split_axis=2, concat_axis=1, tiled=True)
         result, extra = local(moved)
-        return (lax.all_to_all(result, HARM, split_axis=1, concat_axis=2, tiled=True), extra)
+        return (register_the_panel(result, HARM), extra)
 
     def operator(field):
         above, below = sides(field)

time: 379 us -> 526 us (1.39)
  local copies, waits for them, and re-layouts: 31.7 us -> 179 us
    unnamed x47 -> x287, local copies, waits for them, and re-layouts: 7.05 us -> 155 us
  transfers between devices with their start and end apart: 16 -> 16, of which waited for: 8 -> 8; matrix products, arithmetic and copies ran while one was open for 7% -> 12% of each run, Pallas kernels for 0% -> 0%
where the time goes in v1:
time: 526 us; the launch traced here: 525 us
  local copies, waits for them, and re-layouts  179 us (34%)
  blocking collectives  159 us (30%)
  starting transfers between devices  77.7 us (15%)
  waiting for transfers between devices  55.9 us (11%)
  other arithmetic  29.1 us (6%)
  between operations  16.3 us (3%)
  matrix products  7.86 us (1%)
    psum x16, blocking collectives, by_axis(): return functools.reduce(lax.psum, axes, shard)  159 us
    unnamed x287, local copies, waits for them, and re-layouts  155 us
    all_to_all x4, waiting for transfers between devices, across(): moved = lax.all_to_all(field, HARM, split_axis=2, concat_axis=1, tiled=True)  41.9 us
    all_to_all x4, starting transfers between devices, across(): moved = lax.all_to_all(field, HARM, split_axis=2, concat_axis=1, tiled=True)  29.3 us
    all_to_all x4, starting transfers between devices, register_the_panel(): lax.all_to_all(jnp.stack(jnp.split(sheet, lax.axis_size(net_axis), axis=1...  24.9 us
    all_to_all x4, waiting for transfers between devices, register_the_panel(): lax.all_to_all(jnp.stack(jnp.split(sheet, lax.axis_size(net_axis), axis=1...  13.9 us
    slice x18, local copies, waits for them, and re-layouts, stencil(): skewed = skewed + picked * jnp.roll(above, -amount, axis=3)  11.9 us
    ppermute x4, starting transfers between devices, extended(): lax.ppermute(head, axis, [((i + 1) % count, i) for i in range(ends)])  11.8 us
  transfers between devices with their start and end apart: 16, of which 8 were waited for; matrix products, arithmetic and copies ran while one was open for 12% of the time, Pallas kernels for 0%

profile of v1, /device:TPU:2, one launch (start us, length us, event | category | flops | bytes accessed | tf_op | source)
XLA Modules:
  0.0 524.5 jit_solution(14891315720565552888)
XLA Ops:
  9.1 12.2 %all-to-all-start = ((f32[2,2,128,128]{3,1,0,2:T(2,128)}), f32[2,2,128,128]{3,1,0,2:T(2,128)S(1)}, u32[]{:S(2)}, u32[]{:S(2)}) async-start(f32[2,2,128,128]{3,1,0,2:T(2,128)} %copy.395), calls=%async_computation | async-start | bytes 524288 | tf_op jit(solution)/shard_map/all_to_all | solution.py:148
  24.8 8.5 %all-to-all-done = f32[2,2,128,128]{3,1,0,2:T(2,128)S(1)} async-done(((f32[2,2,128,128]{3,1,0,2:T(2,128)}), f32[2,2,128,128]{3,1,0,2:T(2,128)S(1)}, u32[]{:S(2)}, u32[]{:S(2)}) %all-to-all-start) | async-done | bytes 262176 | tf_op jit(solution)/shard_map/all_to_all | solution.py:148
  72.4 6.0 %all-to-all-start.1 = ((f32[64,2,2,2,128]{4,3,2,1,0:T(2,128)}), f32[64,2,2,2,128]{4,3,2,1,0:T(2,128)S(1)}, u32[]{:S(2)}, u32[]{:S(2)}) async-start(f32[64,2,2,2,128]{4,3,2,1,0:T(2,128)} %constant_dynamic-update-slice_fusion), calls=%async_computation.1 | async-start | bytes 524288 | tf_op jit(solution)/shard_map/all_to_all | solution.py:19
  79.6 10.9 %all-to-all-done.1 = f32[64,2,2,2,128]{4,3,2,1,0:T(2,128)S(1)} async-done(((f32[64,2,2,2,128]{4,3,2,1,0:T(2,128)}), f32[64,2,2,2,128]{4,3,2,1,0:T(2,128)S(1)}, u32[]{:S(2)}, u32[]{:S(2)}) %all-to-all-start.1) | async-done | bytes 262176 | tf_op jit(solution)/shard_map/all_to_all | solution.py:19
  93.5 10.9 %psum.196 = f32[]{:T(128)} all-reduce(f32[]{:T(128)} %get-tuple-element.41), channel_id=1, replica_groups=mesh['harm_0'=4,'harm_1'=8,'harm_2'=2,'node'=4] {'harm_0'}, use_global_device_ids=true, to_apply=%region_1.2 | all-reduce | flops 1 | bytes 8 | tf_op jit(solution)/shard_map/psum | solution.py:44
  104.4 15.5 %psum.197 = f32[]{:T(128)} all-reduce(f32[]{:T(128)} %psum.196), channel_id=1, replica_groups=mesh['harm_0'=4,'harm_1'=8,'harm_2'=2,'node'=4] {'harm_1'}, use_global_device_ids=true, to_apply=%region_2.3 | all-reduce | flops 1 | bytes 8 | tf_op jit(solution)/shard_map/psum | solution.py:44
  123.0 9.2 %psum.199 = f32[]{:T(128)} all-reduce(f32[]{:T(128)} %psum.198), channel_id=1, replica_groups=mesh['harm_0'=4,'harm_1'=8,'harm_2'=2,'node'=4] {'node'}, use_global_device_ids=true, to_apply=%region_4.5 | all-reduce | flops 1 | bytes 8 | tf_op jit(solution)/shard_map/psum | solution.py:44
  136.4 5.7 %all-to-all-start.2 = ((f32[2,2,128,128]{3,1,0,2:T(2,128)}), f32[2,2,128,128]{3,1,0,2:T(2,128)S(1)}, u32[]{:S(2)}, u32[]{:S(2)}) async-start(f32[2,2,128,128]{3,1,0,2:T(2,128)} %copy.398), calls=%async_computation.2 | async-start | bytes 524288 | tf_op jit(solution)/shard_map/all_to_all | solution.py:148
  142.2 11.8 %all-to-all-done.2 = f32[2,2,128,128]{3,1,0,2:T(2,128)S(1)} async-done(((f32[2,2,128,128]{3,1,0,2:T(2,128)}), f32[2,2,128,128]{3,1,0,2:T(2,128)S(1)}, u32[]{:S(2)}, u32[]{:S(2)}) %all-to-all-start.2) | async-done | bytes 262176 | tf_op jit(solution)/shard_map/all_to_all | solution.py:148
  193.1 6.0 %all-to-all-start.3 = ((f32[64,2,2,2,128]{4,3,2,1,0:T(2,128)}), f32[64,2,2,2,128]{4,3,2,1,0:T(2,128)S(1)}, u32[]{:S(2)}, u32[]{:S(2)}) async-start(f32[64,2,2,2,128]{4,3,2,1,0:T(2,128)} %constant_dynamic-update-slice_fusion.64), calls=%async_computation.3 | async-start | bytes 524288 | tf_op jit(solution)/shard_map/all_to_all | solution.py:19
  214.6 11.0 %all-reduce.8 = (f32[]{:T(128)}, f32[1]{0:T(128)}) all-reduce(f32[]{:T(128)} %get-tuple-element.10, f32[1]{0:T(128)} %bitcast.152), channel_id=1, replica_groups=mesh['harm_0'=4,'harm_1'=8,'harm_2'=2,'node'=4] {'harm_0'}, use_global_device_ids=true, to_apply=%region_11.12 | all-reduce | flops 2 | bytes 16 | tf_op jit(solution)/shard_map/psum | solution.py:44
  225.6 17.0 %all-reduce.2 = (f32[]{:T(128)}, f32[1]{0:T(128)}) all-reduce(f32[]{:T(128)} %get-tuple-element.31, f32[1]{0:T(128)} %get-tuple-element.32), channel_id=1, replica_groups=mesh['harm_0'=4,'harm_1'=8,'harm_2'=2,'node'=4] {'harm_1'}, use_global_device_ids=true, to_apply=%region_12.13 | all-reduce | flops 2 | bytes 16 | tf_op jit(solution)/shard_map/psum | solution.py:44
  245.8 9.2 %all-reduce.5 = (f32[]{:T(128)}, f32[1]{0:T(128)}) all-reduce(f32[]{:T(128)} %get-tuple-element.37, f32[1]{0:T(128)} %get-tuple-element.38), channel_id=1, replica_groups=mesh['harm_0'=4,'harm_1'=8,'harm_2'=2,'node'=4] {'node'}, use_global_device_ids=true, to_apply=%region_14.15 | all-reduce | flops 2 | bytes 16 | tf_op jit(solution)/shard_map/psum | solution.py:44
  265.8 11.8 %all-to-all-done.4 = f32[2,2,128,128]{3,1,0,2:T(2,128)S(1)} async-done(((f32[2,2,128,128]{3,1,0,2:T(2,128)}), f32[2,2,128,128]{3,1,0,2:T(2,128)S(1)}, u32[]{:S(2)}, u32[]{:S(2)}) %all-to-all-start.4) | async-done | bytes 262176 | tf_op jit(solution)/shard_map/all_to_all | solution.py:148
  316.7 6.3 %all-to-all-start.5 = ((f32[64,2,2,2,128]{4,3,2,1,0:T(2,128)}), f32[64,2,2,2,128]{4,3,2,1,0:T(2,128)}, u32[]{:S(2)}, u32[]{:S(2)}) async-start(f32[64,2,2,2,128]{4,3,2,1,0:T(2,128)} %constant_dynamic-update-slice_fusion.128), calls=%async_computation.5 | async-start | bytes 524288 | tf_op jit(solution)/shard_map/all_to_all | solution.py:19
  340.4 11.0 %all-reduce.7 = (f32[]{:T(128)}, f32[2]{0:T(128)S(1)}) all-reduce(f32[]{:T(128)} %get-tuple-element.7, f32[2]{0:T(128)S(1)} %pad_maximum_fusion.22), channel_id=1, replica_groups=mesh['harm_0'=4,'harm_1'=8,'harm_2'=2,'node'=4] {'harm_0'}, use_global_device_ids=true, to_apply=%region_22.23 | all-reduce | flops 3 | bytes 24 | tf_op jit(solution)/shard_map/psum | solution.py:44
  351.4 17.6 %all-reduce.1 = (f32[]{:T(128)}, f32[2]{0:T(128)S(1)}) all-reduce(f32[]{:T(128)} %get-tuple-element.29, f32[2]{0:T(128)S(1)} %get-tuple-element.30), channel_id=1, replica_groups=mesh['harm_0'=4,'harm_1'=8,'harm_2'=2,'node'=4] {'harm_1'}, use_global_device_ids=true, to_apply=%region_23.24 | all-reduce | flops 3 | bytes 24 | tf_op jit(solution)/shard_map/psum | solution.py:44
  372.1 8.0 %all-reduce.4 = (f32[]{:T(128)}, f32[2]{0:T(128)S(1)}) all-reduce(f32[]{:T(128)} %get-tuple-element.35, f32[2]{0:T(128)S(1)} %get-tuple-element.36), channel_id=1, replica_groups=mesh['harm_0'=4,'harm_1'=8,'harm_2'=2,'node'=4] {'node'}, use_global_device_ids=true, to_apply=%region_25.26 | all-reduce | flops 3 | bytes 24 | tf_op jit(solution)/shard_map/psum | solution.py:44
  387.5 5.8 %all-to-all-start.6 = ((f32[2,2,128,128]{3,1,0,2:T(2,128)}), f32[2,2,128,128]{3,1,0,2:T(2,128)S(1)}, u32[]{:S(2)}, u32[]{:S(2)}) async-start(f32[2,2,128,128]{3,1,0,2:T(2,128)} %copy.404), calls=%async_computation.6 | async-start | bytes 524288 | tf_op jit(solution)/shard_map/all_to_all | solution.py:148
  395.5 9.7 %all-to-all-done.6 = f32[2,2,128,128]{3,1,0,2:T(2,128)S(1)} async-done(((f32[2,2,128,128]{3,1,0,2:T(2,128)}), f32[2,2,128,128]{3,1,0,2:T(2,128)S(1)}, u32[]{:S(2)}, u32[]{:S(2)}) %all-to-all-start.6) | async-done | bytes 262176 | tf_op jit(solution)/shard_map/all_to_all | solution.py:148
  444.4 6.5 %all-to-all-start.7 = ((f32[64,2,2,2,128]{4,3,2,1,0:T(2,128)}), f32[64,2,2,2,128]{4,3,2,1,0:T(2,128)}, u32[]{:S(2)}, u32[]{:S(2)}) async-start(f32[64,2,2,2,128]{4,3,2,1,0:T(2,128)} %constant_dynamic-update-slice_fusion.192), calls=%async_computation.7 | async-start | bytes 524288 | tf_op jit(solution)/shard_map/all_to_all | solution.py:19
  468.1 10.9 %all-reduce.6 = (f32[]{:T(128)}, f32[3]{0:T(128)S(1)}) all-reduce(f32[]{:T(128)} %get-tuple-element.3, f32[3]{0:T(128)S(1)} %pad_maximum_fusion.23), channel_id=1, replica_groups=mesh['harm_0'=4,'harm_1'=8,'harm_2'=2,'node'=4] {'harm_0'}, use_global_device_ids=true, to_apply=%region_35.36 | all-reduce | flops 4 | bytes 32 | tf_op jit(solution)/shard_map/psum | solution.py:44
  479.0 16.1 %all-reduce = (f32[]{:T(128)}, f32[3]{0:T(128)S(1)}) all-reduce(f32[]{:T(128)} %get-tuple-element.27, f32[3]{0:T(128)S(1)} %get-tuple-element.28), channel_id=1, replica_groups=mesh['harm_0'=4,'harm_1'=8,'harm_2'=2,'node'=4] {'harm_1'}, use_global_device_ids=true, to_apply=%region_36.37 | all-reduce | flops 4 | bytes 32 | tf_op jit(solution)/shard_map/psum | solution.py:44
  498.1 10.2 %all-reduce.3 = (f32[]{:T(128)}, f32[3]{0:T(128)S(1)}) all-reduce(f32[]{:T(128)} %get-tuple-element.33, f32[3]{0:T(128)S(1)} %get-tuple-element.34), channel_id=1, replica_groups=mesh['harm_0'=4,'harm_1'=8,'harm_2'=2,'node'=4] {'node'}, use_global_device_ids=true, to_apply=%region_38.39 | all-reduce | flops 4 | bytes 32 | tf_op jit(solution)/shard_map/psum | solution.py:44
  (430 shorter events, 260.2 us)
Async XLA Ops:
  1.4 23.2 %collective-permute-start = (f32[2,2,1,128]{3,2,1,0:T(1,128)S(1)}, f32[2,2,1,128]{3,2,1,0:T(1,128)S(1)}, u32[]{:S(2)}, u32[]{:S(2)}) collective-permute-start(f32[2,2,1,128]{3,2,1,0:T(1,128)S(1)} %get-tuple-element.69), channel_id=1, source_target_pairs={{0,1},{1,2},{2,3},{4,5},{5,6},{6,7},{8,9},{9,10},{10,11},{12,13},{... | collective-permute-start | bytes 6152 | tf_op jit(solution)/shard_map/ppermute | solution.py:34
  4.8 85.8 %collective-permute-start.1 = (f32[2,2,1,128]{3,2,1,0:T(1,128)S(1)}, f32[2,2,1,128]{3,2,1,0:T(1,128)S(1)}, u32[]{:S(2)}, u32[]{:S(2)}) collective-permute-start(f32[2,2,1,128]{3,2,1,0:T(1,128)S(1)} %get-tuple-element.70), channel_id=1, source_target_pairs={{1,0},{2,1},{3,2},{5,4},{6,5},{7,6},{9,8},{10,9},{11,10},{13,12},{... | collective-permute-start | bytes 6152 | tf_op jit(solution)/shard_map/ppermute | solution.py:36
  9.1 12.3 %copy-start.14 = (f32[3,4]{1,0:T(4,128)S(1)}, f32[3,4]{1,0:T(4,128)}, u32[]{:S(2)}) copy-start(f32[3,4]{1,0:T(4,128)} %param.12) | copy-start | bytes 148
  9.1 24.2 %all-to-all-start = ((f32[2,2,128,128]{3,1,0,2:T(2,128)}), f32[2,2,128,128]{3,1,0,2:T(2,128)S(1)}, u32[]{:S(2)}, u32[]{:S(2)}) async-start(f32[2,2,128,128]{3,1,0,2:T(2,128)} %copy.395), calls=%async_computation | async-start | bytes 524288 | tf_op jit(solution)/shard_map/all_to_all | solution.py:148
  21.3 1.6 copy-start
  72.4 18.0 %all-to-all-start.1 = ((f32[64,2,2,2,128]{4,3,2,1,0:T(2,128)}), f32[64,2,2,2,128]{4,3,2,1,0:T(2,128)S(1)}, u32[]{:S(2)}, u32[]{:S(2)}) async-start(f32[64,2,2,2,128]{4,3,2,1,0:T(2,128)} %constant_dynamic-update-slice_fusion), calls=%async_computation.1 | async-start | bytes 524288 | tf_op jit(solution)/shard_map/all_to_all | solution.py:19
  93.5 370.3 %copy-start.1 = (f32[2,2,128,128]{3,2,1,0:T(8,128)}, f32[2,2,128,128]{3,2,1,0:T(8,128)S(1)}, u32[]{:S(2)}) copy-start(f32[2,2,128,128]{3,2,1,0:T(8,128)S(1)} %get-tuple-element.42) | copy-start | bytes 786436
  136.4 17.6 %all-to-all-start.2 = ((f32[2,2,128,128]{3,1,0,2:T(2,128)}), f32[2,2,128,128]{3,1,0,2:T(2,128)S(1)}, u32[]{:S(2)}, u32[]{:S(2)}) async-start(f32[2,2,128,128]{3,1,0,2:T(2,128)} %copy.398), calls=%async_computation.2 | async-start | bytes 524288 | tf_op jit(solution)/shard_map/all_to_all | solution.py:148
  193.1 18.0 %all-to-all-start.3 = ((f32[64,2,2,2,128]{4,3,2,1,0:T(2,128)}), f32[64,2,2,2,128]{4,3,2,1,0:T(2,128)S(1)}, u32[]{:S(2)}, u32[]{:S(2)}) async-start(f32[64,2,2,2,128]{4,3,2,1,0:T(2,128)} %constant_dynamic-update-slice_fusion.64), calls=%async_computation.3 | async-start | bytes 524288 | tf_op jit(solution)/shard_map/all_to_all | solution.py:19
  199.2 7.0 %collective-permute-start.2 = (f32[2,2,1,128]{3,2,1,0:T(1,128)S(1)}, f32[2,2,1,128]{3,2,1,0:T(1,128)S(1)}, u32[]{:S(2)}, u32[]{:S(2)}) collective-permute-start(f32[2,2,1,128]{3,2,1,0:T(1,128)S(1)} %get-tuple-element.61), channel_id=1, source_target_pairs={{0,1},{1,2},{2,3},{4,5},{5,6},{6,7},{8,9},{9,10},{10,11},{12,13},{... | collective-permute-start | bytes 6152 | tf_op jit(solution)/shard_map/ppermute | solution.py:34
  203.2 8.0 %collective-permute-start.3 = (f32[2,2,1,128]{3,2,1,0:T(1,128)S(1)}, f32[2,2,1,128]{3,2,1,0:T(1,128)S(1)}, u32[]{:S(2)}, u32[]{:S(2)}) collective-permute-start(f32[2,2,1,128]{3,2,1,0:T(1,128)S(1)} %get-tuple-element.62), channel_id=1, source_target_pairs={{1,0},{2,1},{3,2},{5,4},{6,5},{7,6},{9,8},{10,9},{11,10},{13,12},{... | collective-permute-start | bytes 6152 | tf_op jit(solution)/shard_map/ppermute | solution.py:36
  260.0 17.6 %all-to-all-start.4 = ((f32[2,2,128,128]{3,1,0,2:T(2,128)}), f32[2,2,128,128]{3,1,0,2:T(2,128)S(1)}, u32[]{:S(2)}, u32[]{:S(2)}) async-start(f32[2,2,128,128]{3,1,0,2:T(2,128)} %copy.401), calls=%async_computation.4 | async-start | bytes 524288 | tf_op jit(solution)/shard_map/all_to_all | solution.py:148
  316.7 18.1 %all-to-all-start.5 = ((f32[64,2,2,2,128]{4,3,2,1,0:T(2,128)}), f32[64,2,2,2,128]{4,3,2,1,0:T(2,128)}, u32[]{:S(2)}, u32[]{:S(2)}) async-start(f32[64,2,2,2,128]{4,3,2,1,0:T(2,128)} %constant_dynamic-update-slice_fusion.128), calls=%async_computation.5 | async-start | bytes 524288 | tf_op jit(solution)/shard_map/all_to_all | solution.py:19
  323.0 6.8 %collective-permute-start.4 = (f32[2,2,1,128]{3,2,1,0:T(1,128)S(1)}, f32[2,2,1,128]{3,2,1,0:T(1,128)S(1)}, u32[]{:S(2)}, u32[]{:S(2)}) collective-permute-start(f32[2,2,1,128]{3,2,1,0:T(1,128)S(1)} %get-tuple-element.55), channel_id=1, source_target_pairs={{0,1},{1,2},{2,3},{4,5},{5,6},{6,7},{8,9},{9,10},{10,11},{12,13},{... | collective-permute-start | bytes 6152 | tf_op jit(solution)/shard_map/ppermute | solution.py:34
  326.1 9.9 %collective-permute-start.5 = (f32[2,2,1,128]{3,2,1,0:T(1,128)S(1)}, f32[2,2,1,128]{3,2,1,0:T(1,128)S(1)}, u32[]{:S(2)}, u32[]{:S(2)}) collective-permute-start(f32[2,2,1,128]{3,2,1,0:T(1,128)S(1)} %get-tuple-element.56), channel_id=1, source_target_pairs={{1,0},{2,1},{3,2},{5,4},{6,5},{7,6},{9,8},{10,9},{11,10},{13,12},{... | collective-permute-start | bytes 6152 | tf_op jit(solution)/shard_map/ppermute | solution.py:36
  334.8 1.1 copy-start.5
  334.8 1.1 copy-start.6
  387.5 17.8 %all-to-all-start.6 = ((f32[2,2,128,128]{3,1,0,2:T(2,128)}), f32[2,2,128,128]{3,1,0,2:T(2,128)S(1)}, u32[]{:S(2)}, u32[]{:S(2)}) async-start(f32[2,2,128,128]{3,1,0,2:T(2,128)} %copy.404), calls=%async_computation.6 | async-start | bytes 524288 | tf_op jit(solution)/shard_map/all_to_all | solution.py:148
  444.4 18.3 %all-to-all-start.7 = ((f32[64,2,2,2,128]{4,3,2,1,0:T(2,128)}), f32[64,2,2,2,128]{4,3,2,1,0:T(2,128)}, u32[]{:S(2)}, u32[]{:S(2)}) async-start(f32[64,2,2,2,128]{4,3,2,1,0:T(2,128)} %constant_dynamic-update-slice_fusion.192), calls=%async_computation.7 | async-start | bytes 524288 | tf_op jit(solution)/shard_map/all_to_all | solution.py:19
  450.9 6.7 %collective-permute-start.6 = (f32[2,2,1,128]{3,2,1,0:T(1,128)S(1)}, f32[2,2,1,128]{3,2,1,0:T(1,128)S(1)}, u32[]{:S(2)}, u32[]{:S(2)}) collective-permute-start(f32[2,2,1,128]{3,2,1,0:T(1,128)S(1)} %get-tuple-element.49), channel_id=1, source_target_pairs={{0,1},{1,2},{2,3},{4,5},{5,6},{6,7},{8,9},{9,10},{10,11},{12,13},{... | collective-permute-start | bytes 6152 | tf_op jit(solution)/shard_map/ppermute | solution.py:34
  454.1 9.8 %collective-permute-start.7 = (f32[2,2,1,128]{3,2,1,0:T(1,128)S(1)}, f32[2,2,1,128]{3,2,1,0:T(1,128)S(1)}, u32[]{:S(2)}, u32[]{:S(2)}) collective-permute-start(f32[2,2,1,128]{3,2,1,0:T(1,128)S(1)} %get-tuple-element.50), channel_id=1, source_target_pairs={{1,0},{2,1},{3,2},{5,4},{6,5},{7,6},{9,8},{10,9},{11,10},{13,12},{... | collective-permute-start | bytes 6152 | tf_op jit(solution)/shard_map/ppermute | solution.py:36
  460.0 3.8 copy-start.13
  462.7 1.1 copy-start.3
  462.7 1.1 copy-start.4
  (9 other events, 8.2 us)
